TPU v7x, 32 devices: a whole 2x2x4 slice. The times are simulated.
32 devices in a mesh: dp: 2 (over x), tp: 16 (over y, z, core).
Axes of the slice: x: 2, y: 2, z: 4, core: 2. Of those that a mesh axis runs over, the one named last changes fastest.
Arguments:
- x: bfloat16 [4096, 7168], P('dp'), parts along dimension 0
- w_gate: bfloat16 [7168, 18432], P(None, 'tp')
- w_up: bfloat16 [7168, 18432], P(None, 'tp')
- w_down: bfloat16 [18432, 7168], P('tp')
Outputs:
- output: bfloat16 [4096, 7168], P('dp'), parts along dimension 0
There are 2 independent parts. A program takes and returns all parts, laid end to end along the dimension named above; an argument that names none is the same for every part.
All inputs are finite; a program needn't handle non-finite values.
Results may differ from a plain program's by a relative error of at most 0.016.
Values are sent between devices in bfloat16 or wider.
A program may use at most 2 GiB of HBM per device.

v0:
```python
import jax
import jax.numpy as jnp
from jax import lax
from jax.sharding import PartitionSpec as P


def solution(mesh):
    def step(x, w_gate, w_up, w_down):
        gate = jnp.dot(x, w_gate, preferred_element_type=jnp.float32)
        up = jnp.dot(x, w_up, preferred_element_type=jnp.float32)
        hidden = (jax.nn.silu(gate) * up).astype(jnp.bfloat16)
        term = jnp.dot(hidden, w_down, preferred_element_type=jnp.float32).astype(jnp.bfloat16)
        return lax.psum(term, "tp")

    return jax.shard_map(
        step,
        mesh=mesh,
        in_specs=(P("dp", None), P(None, "tp"), P(None, "tp"), P("tp", None)),
        out_specs=P("dp", None),
        check_vma=False,
    )
```

profile of v0, /device:TPU:0, one launch (start us, length us, event | category | flops | bytes accessed | tf_op | source)
XLA Modules:
  0.0 674.7 jit_solution(16284900468770997508)
XLA Ops:
  6.5 0.0 all-reduce.2.cloned.1.call-start
  6.5 44.9 %fusion.1 = f32[2048,1152]{1,0:T(8,128)S(1)} fusion(bf16[2048,7168]{1,0:T(8,128)(2,1)} %param.4, bf16[7168,1152]{1,0:T(8,128)(2,1)} %param.5), kind=kOutput, calls=%fused_computation.3 | convolution fusion | flops 33822867456 | bytes 55312384 | tf_op jit(solution)/shard_map/dot_general | solution.py:9
  51.4 47.8 %fusion = bf16[2048,1152]{1,0:T(8,128)(2,1)} fusion(bf16[2048,7168]{1,0:T(8,128)(2,1)} %param.4, bf16[7168,1152]{1,0:T(8,128)(2,1)} %param.6, f32[2048,1152]{1,0:T(8,128)S(1)} %fusion.1), kind=kOutput, calls=%fused_computation.2 | convolution fusion | flops 33837023232 | bytes 60030976 | tf_op jit(solution)/shard_map/dot_general | solution.py:10
  99.2 45.5 %convolution_convert_fusion = bf16[2048,7168]{1,0:T(8,128)(2,1)} fusion(bf16[2048,1152]{1,0:T(8,128)(2,1)} %fusion, bf16[1152,7168]{1,0:T(8,128)(2,1)} %param.7), kind=kOutput, calls=%fused_computation | convolution fusion | flops 33837547520 | bytes 50593792 | tf_op jit(solution)/shard_map/dot_general | solution.py:12
  144.8 0.0 all-reduce.2.cloned.1.call-update
  144.8 502.9 %all-reduce.2.cloned.1.call-done = bf16[2048,7168]{1,0:T(8,128)(2,1)} async-done(((bf16[2048,7168]{1,0:T(8,128)(2,1)}), bf16[2048,7168]{1,0:T(8,128)(2,1)}) %all-reduce.2.cloned.1.call-update) | async-done | bytes 29360144 | tf_op jit(solution)/shard_map/psum | solution.py:13
  647.7 20.1 %copy.6 = bf16[2048,7168]{1,0:T(8,128)(2,1)} copy(bf16[2048,7168]{1,0:T(8,128)(2,1)} %all-reduce.2.cloned.1.call-done) | data formatting | bytes 58720256
Async XLA Ops:
  6.5 641.2 %all-reduce.2.cloned.1.call-start = ((), (), s32[]{:S(2)}) async-start(), calls=%async_computation | async-start | bytes 58720256 | tf_op jit(solution)/shard_map/psum | solution.py:13
Sparse Core Ops, SparseCore 0:
  144.9 502.7 all-reduce.1
where the time goes:
time: 675 us
  waiting for transfers between devices  503 us (75%)
  matrix products  138 us (20%)
  local copies, waits for them, and re-layouts  20.1 us (3%)
  between operations  13.4 us (2%)
    psum x1, waiting for transfers between devices, step(): return lax.psum(term, 'tp')  503 us
    dot_general x1, matrix products, step(): up = jnp.dot(x, w_up, preferred_element_type=jnp.float32)  47.8 us
    dot_general x1, matrix products, step(): jnp.dot(hidden, w_down, preferred_element_type=jnp.float32)  45.5 us
    dot_general x1, matrix products, step(): gate = jnp.dot(x, w_gate, preferred_element_type=jnp.float32)  44.9 us
    unnamed x1, local copies, waits for them, and re-layouts  20.1 us
  transfers between devices with their start and end apart: 1, of which 1 were waited for; matrix products, arithmetic and copies ran while one was open for 0% of the time, Pallas kernels for 0%

commit v1 on v0

v1 whole, which is shorter than its diff:
```python
import functools

import jax
import jax.numpy as jnp
from jax import lax
from jax.experimental import pallas as pl
from jax.experimental.pallas import tpu as pltpu
from jax.sharding import PartitionSpec as P

MESH = pl.DeviceIdType.MESH
F32, BF16 = jnp.float32, jnp.bfloat16

CH = 256
HALF = CH // 2
TN = 1024
KB = 1024
RAIL = 384
COMB = TN - RAIL
SLAB = 2 * RAIL + COMB
NB = 2
W = 4
WD = 8
WA = 8
LAST = 11
PARTS = 8


def kernel(x, wg, wu, wd, out, xb, wgu, wdb, acc, hid, part, psend, precv, gsend, grecv, ls, lra, lrb, xs, xr,
           sem_load, sem_wd, s_pair, r_pair, s_rung, r_rung, s_rs, r_a, r_b, s_x, r_x, s_c, r_c, s_r, r_r, s_g, r_g, s_d, r_d):
    rows, d = x.shape
    f = wg.shape[1]
    nt, nk, nch = d // TN, d // KB, rows // CH
    n = nt * nch
    div, rem = lax.div, lax.rem

    dp, tp = lax.axis_index("dp"), lax.axis_index("tp")
    y, z, c = div(tp, 8), rem(div(tp, 2), 4), rem(tp, 2)
    inner = jnp.logical_and(z >= 1, z <= 2)
    outer = jnp.logical_not(inner)
    low = z <= 1
    near = jnp.where(low, 0, 3)
    adj = jnp.where(low, 1, 2)
    opp = 3 - adj
    far = 3 - near

    def dev(yy, zz, cc):
        return (dp, (yy * 4 + zz) * 2 + cc)

    partner, rung = dev(y, z, 1 - c), dev(1 - y, z, c)
    to_adj, to_near, to_opp = dev(y, adj, c), dev(y, near, c), dev(y, opp, c)

    def remote(src, dst, ss, rs, to):
        return pltpu.make_async_remote_copy(src_ref=src, dst_ref=dst, send_sem=ss, recv_sem=rs, device_id=to, device_id_type=MESH)

    def loads(g):
        slot, b, j = rem(g, NB), rem(g, nk), div(g, nk)
        k0 = pl.ds(pl.multiple_of(b * KB, KB), KB)
        own = pl.ds(pl.multiple_of(j * CH + c * HALF, HALF), HALF)
        oth = pl.ds(pl.multiple_of(j * CH + (1 - c) * HALF, HALF), HALF)
        return (
            pltpu.make_async_copy(wg.at[k0, :], wgu.at[slot, :, pl.ds(0, f)], sem_load.at[slot, 0]),
            pltpu.make_async_copy(wu.at[k0, :], wgu.at[slot, :, pl.ds(f, f)], sem_load.at[slot, 1]),
            pltpu.make_async_copy(x.at[own, k0], xb.at[slot, pl.ds(0, HALF)], sem_load.at[slot, 2]),
            pltpu.make_async_copy(x.at[oth, k0], xb.at[slot, pl.ds(HALF, HALF)], sem_load.at[slot, 3]),
        )

    def load_wd(s):
        return pltpu.make_async_copy(wd.at[:, pl.ds(pl.multiple_of(rem(s, nt) * TN, TN), TN)], wdb.at[rem(s, 2)], sem_wd.at[rem(s, 2)])

    for g in range(NB):
        for cp in loads(jnp.int32(g)):
            cp.start()

    barrier = pltpu.get_barrier_semaphore()
    pl.semaphore_signal(barrier, 1, device_id=partner, device_id_type=MESH)
    pl.semaphore_signal(barrier, 1, device_id=rung, device_id_type=MESH)

    @pl.when(outer)
    def _():
        pl.semaphore_signal(barrier, 1, device_id=to_adj, device_id_type=MESH)
        pl.semaphore_wait(barrier, 3)

    @pl.when(inner)
    def _():
        pl.semaphore_signal(barrier, 1, device_id=to_near, device_id_type=MESH)
        pl.semaphore_signal(barrier, 1, device_id=to_opp, device_id_type=MESH)
        pl.semaphore_wait(barrier, 4)

    def gate_up(s, lo, hi):
        g = s + nk
        slot, b = rem(g, NB), rem(g, nk)

        @pl.when(g < nk * nch)
        def _():
            if lo == 0:
                for cp in loads(g):
                    cp.wait()
            for q in range(lo, hi):
                cs = slice(256 * q, 256 * (q + 1))
                r = jnp.dot(xb[slot], wgu[slot, :, cs], preferred_element_type=F32)
                acc[:, cs] = jnp.where(b == 0, 0.0, acc[:, cs]) + r
            if hi == 2 * f // 256:

                @pl.when(b == nk - 1)
                def _():
                    hs = rem(div(g, nk), 2)

                    def one(i, carry):
                        rs = pl.ds(pl.multiple_of(i * 16, 16), 16)
                        gate, up = acc[rs, :f], acc[rs, f:]
                        hid[hs, rs, :] = (jax.nn.silu(gate) * up).astype(BF16)
                        return carry

                    lax.fori_loop(0, CH // 16, one, 0)

                @pl.when(g + NB < nk * nch)
                def _():
                    for cp in loads(g + NB):
                        cp.start()

    def down(s, lo, hi):
        @pl.when(jnp.logical_and(s >= 0, s < n))
        def _():
            if lo == 0:
                load_wd(s).wait()
            hs = rem(div(s, nt), 2)
            for q in range(lo, hi):
                cs = slice(256 * q, 256 * (q + 1))
                r = jnp.dot(hid[hs], wdb[rem(s, 2), :, cs], preferred_element_type=F32)
                part[rem(s, WA), :, cs] = r[:HALF]
                psend[rem(s, 2), :, cs] = r[HALF:].astype(BF16)
            if hi == TN // 256:
                pair(s).start()

    def pair(p):
        return remote(psend.at[rem(p, 2)], precv.at[rem(p, W)], s_pair.at[rem(p, 2)], r_pair.at[rem(p, W)], partner)

    def rung_rs(p):
        return remote(gsend.at[rem(p, W)], grecv.at[rem(p, W)], s_rung.at[rem(p, W)], r_rung.at[rem(p, W)], rung)

    def rs(p, i, dst, sem, j, to):
        w = rem(p, W)
        return remote(ls.at[w, i], dst.at[w, j], s_rs.at[w, i], sem.at[w, j], to)

    def exch(p):
        w = rem(p, W)
        return remote(xs.at[w], xr.at[w], s_x.at[w], r_x.at[w], rung)

    def origin(p):
        return div(p, nt) * CH + c * HALF, rem(p, nt) * TN

    def comb_at(p, k):
        r0, c0 = origin(p)
        return out.at[pl.ds(pl.multiple_of(r0 + 64 * y + 16 * k, 16), 16), pl.ds(pl.multiple_of(c0 + RAIL, 128), COMB)]

    def rail_at(p, k):
        r0, c0 = origin(p)
        return out.at[pl.ds(pl.multiple_of(r0 + 32 * k, 32), 32), pl.ds(pl.multiple_of(c0, 128), RAIL)]

    def ag(at, ss, rs_, p, k, i, j, to):
        w = rem(p, W)
        return remote(at(p, k), at(p, k), ss.at[w, i], rs_.at[w, j], to)

    def rung_ag(p):
        r0, c0 = origin(p)
        ref = out.at[pl.ds(pl.multiple_of(r0 + 64 * y, 64), 64), pl.ds(pl.multiple_of(c0 + RAIL, 128), COMB)]
        return remote(ref, ref, s_g.at[rem(p, W)], r_g.at[rem(p, W)], rung)

    def core_ag(p):
        r0, c0 = origin(p)
        ref = out.at[pl.ds(pl.multiple_of(r0, HALF), HALF), pl.ds(pl.multiple_of(c0, 128), TN)]
        return remote(ref, ref, s_d.at[rem(p, WD)], r_d.at[rem(p, WD)], partner)

    def pieces(k):
        yield slice(0, RAIL), pl.ds(pl.multiple_of(32 * k, 16), 16), slice(0, RAIL)
        yield slice(RAIL, 2 * RAIL), pl.ds(pl.multiple_of(32 * k + 16, 16), 16), slice(0, RAIL)
        yield slice(2 * RAIL, SLAB), pl.ds(pl.multiple_of(64 * y + 16 * k, 16), 16), slice(RAIL, TN)

    def emit(p, k, i, src=None):
        w, a = rem(p, W), rem(p, WA)
        for cs, rw, cl in pieces(k):
            v = part[a, rw, cl]
            if src is not None:
                v = v + src[:, cs].astype(F32)
            ls[w, i, :, cs] = v.astype(BF16)

    def accumulate(p, k, src):
        a = rem(p, WA)
        for cs, rw, cl in pieces(k):
            part[a, rw, cl] = part[a, rw, cl] + src[:, cs].astype(F32)

    def root(p, src):
        w, a = rem(p, W), rem(p, WA)
        for i, (cs, rw, cl) in enumerate(pieces(z)):
            v = (part[a, rw, cl] + src[:, cs].astype(F32)).astype(BF16)
            if i < 2:
                xs[w, 16 * i : 16 * (i + 1), :] = v
            else:
                comb_at(p, z)[...] = v
        exch(p).start()

    def rail_final(p):
        w = rem(p, W)
        exch(p).wait()
        rail_at(p, z)[...] = (xs[w].astype(F32) + xr[w].astype(F32)).astype(BF16)

    def st1(p):
        pair(p).wait_recv()
        a, w = rem(p, WA), rem(p, W)
        for r in range(0, HALF, 16):
            rw = slice(r, r + 16)
            part[a, rw, :RAIL] = part[a, rw, :RAIL] + precv[w, rw, :RAIL].astype(F32)
        for r in range(0, 64, 16):
            mine = pl.ds(pl.multiple_of(64 * y + r, 16), 16)
            other = pl.ds(pl.multiple_of(64 * (1 - y) + r, 16), 16)
            gsend[w, r : r + 16, :] = (part[a, other, RAIL:] + precv[w, other, RAIL:].astype(F32)).astype(BF16)
            part[a, mine, RAIL:] = part[a, mine, RAIL:] + precv[w, mine, RAIL:].astype(F32)
        rung_rs(p).start()

    def st2(p):
        pair(p).wait_send()
        rung_rs(p).wait_recv()
        a, w = rem(p, WA), rem(p, W)
        for r in range(0, 64, 16):
            mine = pl.ds(pl.multiple_of(64 * y + r, 16), 16)
            part[a, mine, RAIL:] = part[a, mine, RAIL:] + grecv[w, r : r + 16, :].astype(F32)

        @pl.when(outer)
        def _():
            for i, k in ((2, far), (1, opp), (0, adj)):
                emit(p, k, i)
                rs(p, i, lra, r_a, i, to_adj).start()

    def st3(p):
        rung_rs(p).wait_send()
        w = rem(p, W)

        @pl.when(inner)
        def _():
            for j, k, i in ((2, far, 1), (1, opp, 0)):
                rs(p, j, lra, r_a, j, to_near).wait_recv()
                emit(p, k, i, lra.at[w, j])
                rs(p, i, lrb, r_b, i, to_opp).start()
            rs(p, 0, lra, r_a, 0, to_near).wait_recv()
            accumulate(p, z, lra.at[w, 0])

    def st4(p):
        w = rem(p, W)

        @pl.when(inner)
        def _():
            rs(p, 1, lrb, r_b, 1, to_opp).wait_recv()
            emit(p, near, 2, lrb.at[w, 1])
            rs(p, 2, lrb, r_b, 0, to_near).start()
            rs(p, 0, lrb, r_b, 0, to_opp).wait_recv()
            root(p, lrb.at[w, 0])
            ag(comb_at, s_c, r_c, p, z, 0, 0, to_near).start()
            ag(comb_at, s_c, r_c, p, z, 1, 0, to_opp).start()

        @pl.when(outer)
        def _():
            for i in range(3):
                rs(p, i, lra, r_a, i, to_adj).wait_send()

    def spread(at, ss, rr, p, q):
        def hop(k, i, j, to):
            return ag(at, ss, rr, p, k, i, j, to)

        if q == 1:

            @pl.when(outer)
            def _():
                hop(z, 0, 1, to_adj).start()
                hop(adj, 0, 0, to_adj).wait_recv()

            @pl.when(inner)
            def _():
                hop(opp, 0, 0, to_opp).wait_recv()
                hop(opp, 2, 1, to_near).start()

        if q == 2:

            @pl.when(inner)
            def _():
                hop(near, 0, 1, to_near).wait_recv()
                hop(near, 3, 2, to_opp).start()
                hop(z, 0, 0, to_near).wait_send()
                hop(z, 1, 0, to_opp).wait_send()

            @pl.when(outer)
            def _():
                hop(opp, 0, 1, to_adj).wait_recv()

        if q == 3:

            @pl.when(inner)
            def _():
                hop(far, 0, 2, to_opp).wait_recv()
                hop(far, 4, 2, to_near).start()
                hop(opp, 2, 1, to_near).wait_send()

            @pl.when(outer)
            def _():
                hop(z, 0, 1, to_adj).wait_send()

        if q == 4:

            @pl.when(outer)
            def _():
                hop(far, 0, 2, to_adj).wait_recv()

            @pl.when(inner)
            def _():
                hop(near, 3, 2, to_opp).wait_send()

        if q == 5:

            @pl.when(inner)
            def _():
                hop(far, 4, 2, to_near).wait_send()

    comb = functools.partial(spread, comb_at, s_c, r_c)
    rail = functools.partial(spread, rail_at, s_r, r_r)

    def st5(p):
        w = rem(p, W)

        @pl.when(outer)
        def _():
            rs(p, 0, lrb, r_b, 0, to_adj).wait_recv()
            root(p, lrb.at[w, 0])

        @pl.when(inner)
        def _():
            for i in range(2):
                rs(p, i, lrb, r_b, i, to_opp).wait_send()
            rail_final(p)
            ag(rail_at, s_r, r_r, p, z, 0, 0, to_near).start()
            ag(rail_at, s_r, r_r, p, z, 1, 0, to_opp).start()

        comb(p, 1)

    def st6(p):
        @pl.when(outer)
        def _():
            rail_final(p)

        @pl.when(inner)
        def _():
            rs(p, 2, lrb, r_b, 0, to_near).wait_send()

        comb(p, 2)
        rail(p, 1)

    def st7(p):
        comb(p, 3)
        rail(p, 2)

    def st8(p):
        comb(p, 4)
        rung_ag(p).start()
        rail(p, 3)

    def st9(p):
        comb(p, 5)
        rail(p, 4)
        rung_ag(p).wait_recv()
        core_ag(p).start()

    def st10(p):
        rail(p, 5)
        rung_ag(p).wait_send()

    def st11(p):
        core_ag(p).wait()

    stages = (None, st1, st2, st3, st4, st5, st6, st7, st8, st9, st10, st11)

    def run(s, qs):
        for q in qs:
            p = s - q

            @pl.when(jnp.logical_and(p >= 0, p < n))
            def _():
                stages[q](p)

    def body(i, carry):
        s = i - nk
        run(s, (1, 2))
        gate_up(s, 0, 3)
        run(s, (3, 4))
        gate_up(s, 3, 6)
        run(s, (5, 6))
        gate_up(s, 6, 9)
        run(s, (7, 8, 9))

        @pl.when(jnp.logical_and(s >= -1, s < n - 1))
        def _():
            load_wd(s + 1).start()

        down(s, 0, 2)
        run(s, (10, 11))
        down(s, 2, 4)
        return carry

    lax.fori_loop(0, nk + n + LAST, body, 0)


def flush(src, dst, sem):
    rows = src.shape[0] // PARTS
    cps = [pltpu.make_async_copy(src.at[pl.ds(i * rows, rows)], dst.at[pl.ds(i * rows, rows)], sem.at[i]) for i in range(PARTS)]
    for cp in cps:
        cp.start()
    for cp in cps:
        cp.wait()


def solution(mesh):
    def step(x, wg, wu, wd):
        rows, d = x.shape
        f = wg.shape[1]
        sem = pltpu.SemaphoreType.DMA
        any_ = pl.BlockSpec(memory_space=pl.ANY)
        whole = pl.pallas_call(
            kernel,
            out_shape=pltpu.VMEM((rows, d), BF16),
            in_specs=[any_] * 4,
            out_specs=pl.BlockSpec(memory_space=pltpu.VMEM),
            scratch_shapes=[
                pltpu.VMEM((NB, CH, KB), BF16),
                pltpu.VMEM((NB, KB, 2 * f), BF16),
                pltpu.VMEM((2, f, TN), BF16),
                pltpu.VMEM((CH, 2 * f), F32),
                pltpu.VMEM((2, CH, f), BF16),
                pltpu.VMEM((WA, HALF, TN), F32),
                pltpu.VMEM((2, HALF, TN), BF16),
                pltpu.VMEM((W, HALF, TN), BF16),
                pltpu.VMEM((W, 64, COMB), BF16),
                pltpu.VMEM((W, 64, COMB), BF16),
                pltpu.VMEM((W, 3, 16, SLAB), BF16),
                pltpu.VMEM((W, 3, 16, SLAB), BF16),
                pltpu.VMEM((W, 2, 16, SLAB), BF16),
                pltpu.VMEM((W, 32, RAIL), BF16),
                pltpu.VMEM((W, 32, RAIL), BF16),
                sem((NB, 4)),
                sem((2,)),
                sem((2,)),
                sem((W,)),
                sem((W,)),
                sem((W,)),
                sem((W, 3)),
                sem((W, 3)),
                sem((W, 2)),
                sem((W,)),
                sem((W,)),
                sem((W, 5)),
                sem((W, 3)),
                sem((W, 5)),
                sem((W, 3)),
                sem((W,)),
                sem((W,)),
                sem((WD,)),
                sem((WD,)),
            ],
            compiler_params=pltpu.CompilerParams(collective_id=0, has_side_effects=True, vmem_limit_bytes=33 * 2**20),
            cost_estimate=pl.CostEstimate(flops=6 * rows * d * f, bytes_accessed=400 * 2**20, transcendentals=rows * f),
        )(x, wg, wu, wd)
        return pl.pallas_call(
            flush,
            out_shape=jax.ShapeDtypeStruct((rows, d), BF16),
            in_specs=[pl.BlockSpec(memory_space=pltpu.VMEM)],
            out_specs=any_,
            scratch_shapes=[sem((PARTS,))],
            compiler_params=pltpu.CompilerParams(vmem_limit_bytes=2**20),
        )(whole)

    return jax.shard_map(
        step,
        mesh=mesh,
        in_specs=(P("dp", None), P(None, "tp"), P(None, "tp"), P("tp", None)),
        out_specs=P("dp", None),
        check_vma=False,
    )
```

time: 675 us -> 320 us (0.47)
  waiting for transfers between devices: 503 us -> 0 us
  Pallas kernels: 0 us -> 320 us
  matrix products: 138 us -> 0 us
  local copies, waits for them, and re-layouts: 20.1 us -> 0 us
  between operations: 13.4 us -> 0.01 us
    psum x1 -> x0, waiting for transfers between devices: 503 us -> none  [step(): return lax.psum(term, 'tp')]
    pallas_call x0 -> x2, Pallas kernels: none -> 320 us  [the longest x1 310 us: step(): pl.pallas_call(kernel, out_shape=pltpu.VMEM((rows, d), BF16), in_specs=[a...]
    dot_general x3 -> x0, matrix products: 138 us -> none  [the longest x1 47.8 us: step(): up = jnp.dot(x, w_up, preferred_element_type=jnp.float32)]
    unnamed x1 -> x0, local copies, waits for them, and re-layouts: 20.1 us -> none
  transfers between devices with their start and end apart: 1 -> 0, of which waited for: 1 -> 0; matrix products, arithmetic and copies ran while one was open for 0% -> 0% of each run, Pallas kernels for 0% -> 0%
where the time goes in v1:
time: 320 us
  Pallas kernels  320 us (100%)
    pallas_call x1, Pallas kernels, step(): pl.pallas_call(kernel, out_shape=pltpu.VMEM((rows, d), BF16), in_specs=[a...  310 us
    pallas_call x1, Pallas kernels, step(): pl.pallas_call(flush, out_shape=jax.ShapeDtypeStruct((rows, d), BF16), in...  9.84 us

profile of v1, /device:TPU:0, one launch (start us, length us, event | category | flops | bytes accessed | tf_op | source)
XLA Modules:
  0.0 319.9 jit_solution(11284188154476444540)
XLA Ops:
  0.0 310.0 %shard_map.46.src = bf16[2048,7168]{1,0:T(8,128)(2,1)S(1)} custom-call(bf16[2048,7168]{1,0:T(8,128)(2,1)} %x.1, bf16[7168,1152]{1,0:T(8,128)(2,1)} %wg.1, bf16[7168,1152]{1,0:T(8,128)(2,1)} %wu.1, bf16[1152,7168]{1,0:T(8,128)(2,1)} %wd.1), custom_call_target="tpu_custom_call" | custom-call | flops 101468602368 | bytes 419430400 | tf_op jit(solution)/shard_map/pallas_call | solution.py:424
  310.0 9.8 %shard_map.47 = bf16[2048,7168]{1,0:T(8,128)(2,1)} custom-call(bf16[2048,7168]{1,0:T(8,128)(2,1)S(1)} %shard_map.46.src), custom_call_target="tpu_custom_call" | custom-call | tf_op jit(solution)/shard_map/pallas_call | solution.py:468
